TPU v7x, 32 devices: a whole 2x2x4 slice. The times are simulated.
32 devices in a mesh: grp: 2 (over x), gx: 4 (over z), gy: 4 (over y, core).
Axes of the slice: x: 2, y: 2, z: 4, core: 2. Of those that a mesh axis runs over, the one named last changes fastest.
Arguments:
- state: float32 [2, 3, 144, 192, 90], P('grp', None, 'gx', 'gy'), may hold values from -6 to 6
- courant: float32 [2, 144, 192, 90], P('grp', 'gx', 'gy'), may hold values from 0.15 to 0.5
- vert_inverse: float32 [2, 90, 90], P('grp'), may hold values from -0.1 to 0.65, as said below
- interp_index: int32 [144, 192, 4], P('gx', 'gy'), may hold values from 0 to 8
- interp_weight: float32 [144, 192, 4], P('gx', 'gy'), may hold values from 0.2 to 1
- restrict_index: int32 [48, 64, 9], P('gx', 'gy'), may hold values from 0 to 8
- restrict_weight: float32 [48, 64, 9], P('gx', 'gy'), may hold values from 0.2 to 1
Outputs:
- new_state: float32 [2, 3, 144, 192, 90], P('grp', None, 'gx', 'gy')
Inputs may be any that keep to these rules, and one draw needn't show every extreme that they name: `vert_inverse`: each matrix's diagonal lies in 0.5 to 0.65, its neighbours on the diagonal beside it in 0.05 to 0.12, the rest is small.
All inputs are finite; a program needn't handle non-finite values.
Results may differ from a plain program's by a relative error of at most 0.0001.
Values sent between devices are 32-bit elements; how exact they have to be, the bound alone decides.
A program may use at most 128 MiB of HBM per device.

v0:
```python
import functools

import jax
import jax.numpy as jnp
from jax import lax
from jax.experimental import pallas as pl
from jax.experimental.pallas import tpu as pltpu
from jax.sharding import PartitionSpec as P

SUBS = 4
BAND = 5
FEEDBACK = 0.5
MESH = pl.DeviceIdType.MESH
F32 = jnp.float32
XB, YB = 2, 8


def split(a):
    high = a.astype(jnp.bfloat16)
    return high, (a - high.astype(F32)).astype(jnp.bfloat16)


def dot(a, b):
    return jnp.dot(a, b, preferred_element_type=F32)


def dot3(a, b_high, b_low):
    a_high, a_low = split(a)
    return dot(a_high, b_high) + (dot(a_low, b_high) + dot(a_high, b_low))


def third(t):
    return (t * 11) >> 5


def dense(cell, share, depth):
    lanes = lax.broadcasted_iota(jnp.int32, (cell.shape[0], depth), 1)
    total = jnp.zeros(lanes.shape, F32)
    for k in range(cell.shape[1]):
        total = total + jnp.where(lanes == cell[:, k : k + 1], share[:, k : k + 1], 0.0)
    return total


def kernel(
    cx, cy,
    state, courant, inverse, iidx, iwgt, ridx, rwgt,
    out,
    S, C, mean, sx0, sy0, rx0, ry0, sx, sy, rx, ry, rst, fb, xstrip, ystrip,
    load_sem, halo_send, halo_recv, strip_send, strip_recv, fb_send, fb_recv, out_sem,
):
    g, a, b = lax.axis_index("grp"), lax.axis_index("gx"), lax.axis_index("gy")
    nx, ny, lev = state.shape[2], state.shape[3], state.shape[4]
    tx, ty = nx // 3, ny // 3
    fx, fy = cx // 2, cy // 2

    loads = [
        pltpu.make_async_copy(
            state.at[0], S.at[:, pl.ds(XB, nx), pl.ds(YB, ny), :], load_sem.at[0]
        ),
        pltpu.make_async_copy(
            courant.at[0], C.at[pl.ds(1, nx), pl.ds(YB, ny), :], load_sem.at[1]
        ),
    ]
    for copy in loads:
        copy.start()
    zrow = jnp.zeros((2, ny, lev), F32)
    S[0, 0:2, YB : YB + ny, :] = zrow
    S[0, XB + nx : XB + nx + 2, YB : YB + ny, :] = zrow
    S[1, 0:2, YB : YB + ny, :] = zrow
    S[1, XB + nx : XB + nx + 2, YB : YB + ny, :] = zrow
    C[0:1, YB : YB + ny, :] = zrow[0:1]
    C[nx + 1 : nx + 2, YB : YB + ny, :] = zrow[0:1]
    zcol = jnp.zeros((nx, 8, lev), F32)
    for c in (0, 2):
        S[c, XB : XB + nx, 0:YB, :] = zcol
        S[c, XB : XB + nx, YB + ny : YB + ny + 8, :] = zcol
    C[1 : 1 + nx, 0:YB, :] = zcol
    C[1 : 1 + nx, YB + ny : YB + ny + 8, :] = zcol
    m_high, m_low = split(inverse[0])
    for copy in loads:
        copy.wait()

    dirs = (
        (a > 0, a < cx - 1, (g, a - 1, b)),
        (a < cx - 1, a > 0, (g, a + 1, b)),
        (b > 0, b < cy - 1, (g, a, b - 1)),
        (b < cy - 1, b > 0, (g, a, b + 1)),
    )

    def halo_copy(k, d):
        if k == 0:
            src, dst = (sx0, rx0) if d < 2 else (sy0, ry0)
            src, dst = src.at[d % 2], dst.at[d % 2]
        else:
            src, dst = (sx, rx) if d < 2 else (sy, ry)
            src, dst = src.at[k - 1, d % 2], dst.at[k - 1, d % 2]
        return pltpu.make_async_remote_copy(
            src_ref=src, dst_ref=dst,
            send_sem=halo_send.at[k, d], recv_sem=halo_recv.at[k, d],
            device_id=dirs[d][2], device_id_type=MESH,
        )

    def exchange(k):
        cols = slice(YB, YB + ny)
        rows = slice(XB, XB + nx)
        last_x, last_y = XB + nx, YB + ny
        if k == 0:
            sx0[0, 0:2] = S[0, XB : XB + 2, cols, :]
            sx0[0, 2:3] = S[1, XB : XB + 1, cols, :]
            sx0[0, 3:4] = C[1:2, cols, :]
            sx0[1, 0:2] = S[0, last_x - 2 : last_x, cols, :]
            sx0[1, 2:3] = S[1, last_x - 1 : last_x, cols, :]
            sx0[1, 3:4] = C[nx : nx + 1, cols, :]
            sy0[0, :, 0:2] = S[0, rows, YB : YB + 2, :]
            sy0[0, :, 2:3] = S[2, rows, YB : YB + 1, :]
            sy0[0, :, 3:4] = C[1 : 1 + nx, YB : YB + 1, :]
            sy0[1, :, 0:2] = S[0, rows, last_y - 2 : last_y, :]
            sy0[1, :, 2:3] = S[2, rows, last_y - 1 : last_y, :]
            sy0[1, :, 3:4] = C[1 : 1 + nx, last_y - 1 : last_y, :]
        else:
            sx[k - 1, 0] = S[0, XB : XB + 2, cols, :]
            sx[k - 1, 1] = S[0, last_x - 2 : last_x, cols, :]
            sy[k - 1, 0] = S[0, rows, YB : YB + 2, :]
            sy[k - 1, 1] = S[0, rows, last_y - 2 : last_y, :]
        for d in range(4):
            @pl.when(dirs[d][0])
            def _():
                halo_copy(k, d).start()
        for d in range(4):
            @pl.when(dirs[d][1])
            def _():
                halo_copy(k, d).wait_recv()
                if d < 2:
                    got = rx0.at[d] if k == 0 else rx.at[k - 1, d]
                    at = last_x if d == 0 else XB - 2
                    S[0, at : at + 2, cols, :] = got[0:2]
                    if k == 0:
                        at = last_x if d == 0 else XB - 1
                        S[1, at : at + 1, cols, :] = got[2:3]
                        C[at - 1 : at, cols, :] = got[3:4]
                else:
                    got = ry0.at[d - 2] if k == 0 else ry.at[k - 1, d - 2]
                    at = last_y if d == 2 else YB - 2
                    S[0, rows, at : at + 2, :] = got[:, 0:2]
                    if k == 0:
                        at = last_y if d == 2 else YB - 1
                        S[2, rows, at : at + 1, :] = got[:, 2:3]
                        C[1 : 1 + nx, at : at + 1, :] = got[:, 3:4]

    def add_mean(k, c, x, value):
        mean[c, x] = value if k == 0 else mean[c, x] + value

    def winds(k):
        def u_row(r, _):
            slope = 0.5 * (S[0, r + 1, YB : YB + ny, :] - S[0, r - 1, YB : YB + ny, :])
            S[1, r, YB : YB + ny, :] = S[1, r, YB : YB + ny, :] - C[r - 1, YB : YB + ny, :] * slope
            return 0

        u_row(XB - 1, 0)
        u_row(XB + nx, 0)

        def row(x, _):
            r = x + XB
            u_row(r, 0)
            add_mean(k, 1, x, S[1, r, YB : YB + ny, :])
            wide = slice(YB - 1, YB + ny + 1)
            slope = 0.5 * (S[0, r, YB : YB + ny + 2, :] - S[0, r, YB - 2 : YB + ny, :])
            S[2, r, wide, :] = S[2, r, wide, :] - C[x + 1, wide, :] * slope
            add_mean(k, 2, x, S[2, r, YB : YB + ny, :])
            return 0

        lax.fori_loop(0, nx, row, 0)

    def press(k):
        group = 4

        def rows(i, _):
            parts = []
            for j in range(group):
                x = i * group + j
                r = x + XB
                div = 0.5 * (S[1, r + 1, YB : YB + ny, :] - S[1, r - 1, YB : YB + ny, :]) + 0.5 * (
                    S[2, r, YB + 1 : YB + ny + 1, :] - S[2, r, YB - 1 : YB + ny - 1, :]
                )
                parts.append(S[0, r, YB : YB + ny, :] - C[x + 1, YB : YB + ny, :] * div)
            solved = dot3(jnp.concatenate(parts, axis=0), m_high, m_low)
            for j in range(group):
                x = i * group + j
                new = solved[j * ny : (j + 1) * ny]
                S[0, x + XB, YB : YB + ny, :] = new
                add_mean(k, 0, x, new)
            return 0

        lax.fori_loop(0, nx // group, rows, 0)

    slot = (a % 3) * 3 + b % 3

    def fb_copy(c):
        return pltpu.make_async_remote_copy(
            src_ref=rst.at[c], dst_ref=fb.at[slot, c],
            send_sem=fb_send.at[c], recv_sem=fb_recv.at[slot, c],
            device_id=(0, fx + a // 3, fy + b // 3), device_id_type=MESH,
        )

    def restrict(comps):
        def row(u, _):
            t = ridx[u]
            w = rwgt[u]
            share = w * (1.0 / SUBS) / jnp.sum(w, axis=-1, keepdims=True)
            over = third(t)
            cell = over * ny + (t - 3 * over) + 3 * lax.broadcasted_iota(jnp.int32, t.shape, 0)
            w_high, w_low = split(dense(cell, share, 3 * ny))
            for c in comps:
                block = mean[c, pl.ds(3 * u, 3)].reshape(3 * ny, lev)
                b_high, b_low = split(block)
                rst[c, u] = dot(w_high, b_high) + (dot(w_low, b_high) + dot(w_high, b_low))
            return 0

        lax.fori_loop(0, tx, row, 0)

    for k in range(SUBS):
        exchange(k)
        winds(k)
        if k == SUBS - 1:
            @pl.when(g == 1)
            def _():
                restrict((1, 2))
                fb_copy(1).start()
                fb_copy(2).start()
        press(k)

    x_windows = {-1: (0, 8, 24), 0: (0, ty + 8, 8), 1: (ty - 8, 2 * ty + 8, 0),
                 2: (2 * ty - 8, ny, 0), 3: (ny - 8, ny, 0)}
    y_windows = {-1: (0, 1, tx + 1), 0: (0, tx + 1, 1), 1: (tx - 1, 2 * tx + 1, 0),
                 2: (2 * tx - 1, nx, 0), 3: (nx - 1, nx, 0)}
    kinds = {-1: 1, 0: 0, 1: 0, 2: 0, 3: 2}

    def strip_copies():
        for side in range(2):
            edge = 0 if side == 0 else cx - 1
            at = XB if side == 0 else XB + tx * (edge % 3) + tx - 3
            for j in range(-1, 4):
                lo, hi, dst = x_windows[j]
                child = 3 * (b - fy) + j
                on = (a == fx + edge // 3) & (b >= fy) & (child >= 0) & (child < cy)
                yield on, pltpu.make_async_remote_copy(
                    src_ref=S.at[:, pl.ds(at, 3), pl.ds(YB + lo, hi - lo), :],
                    dst_ref=xstrip.at[:, :, pl.ds(dst, hi - lo), :],
                    send_sem=strip_send.at[0, side, j + 1], recv_sem=strip_recv.at[0, kinds[j]],
                    device_id=(1, edge, child), device_id_type=MESH,
                )
            edge = 0 if side == 0 else cy - 1
            at = YB if side == 0 else YB + ty * (edge % 3) + ty - 8
            for i in range(-1, 4):
                lo, hi, dst = y_windows[i]
                child = 3 * (a - fx) + i
                on = (b == fy + edge // 3) & (a >= fx) & (child >= 0) & (child < cx)
                yield on, pltpu.make_async_remote_copy(
                    src_ref=S.at[:, pl.ds(XB + lo, hi - lo), pl.ds(at, 8), :],
                    dst_ref=ystrip.at[:, pl.ds(dst, hi - lo), :, :],
                    send_sem=strip_send.at[1, side, i + 1], recv_sem=strip_recv.at[1, kinds[i]],
                    device_id=(1, child, edge), device_id_type=MESH,
                )

    def strip_wait(axis, kind, lo, hi, dst):
        if axis == 0:
            ref = xstrip.at[:, :, pl.ds(dst, hi - lo), :]
        else:
            ref = ystrip.at[:, pl.ds(dst, hi - lo), :, :]
        pltpu.make_async_remote_copy(
            src_ref=ref, dst_ref=ref, send_sem=strip_send.at[0, 0, 0],
            recv_sem=strip_recv.at[axis, kind], device_id=(g, a, b), device_id_type=MESH,
        ).wait_recv()

    def wait_strips(axis, place, count, windows):
        for i in range(3):
            @pl.when(place % 3 == i)
            def _():
                strip_wait(axis, 0, *windows[i])

        @pl.when((place % 3 == 2) & (place < count - 1))
        def _():
            strip_wait(axis, 1, *windows[-1])

        @pl.when((place % 3 == 0) & (place > 0))
        def _():
            strip_wait(axis, 2, *windows[3])

    def relax_at(x, y):
        gx, gy = a * nx + x, b * ny + y
        depth = jnp.minimum(
            jnp.minimum(gx, nx * cx - 1 - gx), jnp.minimum(gy, ny * cy - 1 - gy)
        ).astype(F32)
        return jnp.maximum(1.0 - depth / BAND, 0.0)

    def shares_of(w):
        return w / jnp.sum(w, axis=-1, keepdims=True)

    def y_edge(col, strip0):
        def row(u, _):
            t = iidx[pl.ds(3 * u, 3), pl.ds(col, 8), :].reshape(24, 4)
            share = shares_of(iwgt[pl.ds(3 * u, 3), pl.ds(col, 8), :].reshape(24, 4))
            over = third(t)
            n = lax.broadcasted_iota(jnp.int32, (24, 4), 0)
            source_x = jnp.clip(a * tx + u + over - 1, 0, cx * tx - 1) - (a * tx + u - 1)
            y = col + (n & 7)
            y3 = (y * 171) >> 9
            source_y = jnp.clip(b * ty + y3 + (t - 3 * over) - 1, 0, cy * ty - 1) - (b * ty + strip0)
            w_high, w_low = split(dense(source_x * 8 + source_y, share, 24))
            n = lax.broadcasted_iota(jnp.int32, (24, lev), 0)
            relax = relax_at(3 * u + (n >> 3), col + (n & 7))
            for c in range(3):
                s_high, s_low = split(ystrip[c, pl.ds(u, 3)].reshape(24, lev))
                bound = dot(w_high, s_high) + (dot(w_low, s_high) + dot(w_high, s_low))
                at = (c, pl.ds(XB + 3 * u, 3), pl.ds(YB + col, 8), slice(None))
                now = S[at].reshape(24, lev)
                S[at] = (now + relax * (bound - now)).reshape(3, 8, lev)
            return 0

        lax.fori_loop(0, tx, row, 0)

    def x_edge(first, strip0):
        def row(i, _):
            x = first + i
            t = iidx[x]
            share = shares_of(iwgt[x])
            over = third(t)
            source_x = jnp.clip(a * tx + x // 3 + over - 1, 0, cx * tx - 1) - (a * tx + strip0)
            y = lax.broadcasted_iota(jnp.int32, (ny, 4), 0)
            y3 = (y * 171) >> 9
            source_y = jnp.clip(b * ty + y3 + (t - 3 * over) - 1, 0, cy * ty - 1) - (b * ty - 8)
            w_high, w_low = split(dense(source_x * (ty + 16) + source_y, share, 3 * (ty + 16)))
            y = lax.broadcasted_iota(jnp.int32, (ny, lev), 0)
            relax = relax_at(x, y)
            for c in range(3):
                s_high, s_low = split(xstrip[c].reshape(3 * (ty + 16), lev))
                bound = dot(w_high, s_high) + (dot(w_low, s_high) + dot(w_high, s_low))
                now = keep[c, i]
                S[c, XB + x, YB : YB + ny, :] = now + relax * (bound - now)
            return 0

        keep = mean
        lax.fori_loop(0, BAND, row, 0)

    @pl.when(g == 1)
    def _():
        restrict((0,))
        fb_copy(0).start()
        x_low, x_high = a == 0, a == cx - 1
        y_low, y_high = b == 0, b == cy - 1

        @pl.when(x_low)
        def _():
            for c in range(3):
                mean[c, 0:BAND] = S[c, XB : XB + BAND, YB : YB + ny, :]

        @pl.when(x_high)
        def _():
            for c in range(3):
                mean[c, 0:BAND] = S[c, XB + nx - BAND : XB + nx, YB : YB + ny, :]

        @pl.when(x_low | x_high)
        def _():
            xstrip_pad = jnp.zeros((3, 3, 8, lev), F32)

            @pl.when(y_low)
            def _():
                xstrip[:, :, 0:8, :] = xstrip_pad

            if (cy - 1) % 3 == 2:

                @pl.when(y_high)
                def _():
                    xstrip[:, :, ty + 8 : ty + 16, :] = xstrip_pad

        @pl.when(y_low | y_high)
        def _():
            @pl.when(x_low)
            def _():
                ystrip[:, 0:1] = jnp.zeros((3, 1, 8, lev), F32)

            if (cx - 1) % 3 == 2:

                @pl.when(x_high)
                def _():
                    ystrip[:, tx + 1 : tx + 2] = jnp.zeros((3, 1, 8, lev), F32)

            wait_strips(1, a, cx, y_windows)

        @pl.when(y_low)
        def _():
            y_edge(0, 0)

        @pl.when(y_high)
        def _():
            y_edge(ny - 8, ty - 8)

        @pl.when(x_low | x_high)
        def _():
            wait_strips(0, b, cy, x_windows)

        @pl.when(x_low)
        def _():
            x_edge(0, 0)

        @pl.when(x_high)
        def _():
            x_edge(nx - BAND, tx - 3)

        for c in range(3):
            fb_copy(c).wait_send()

    @pl.when(g == 0)
    def _():
        for on, copy in strip_copies():
            @pl.when(on)
            def _():
                copy.start()
        for on, copy in strip_copies():
            @pl.when(on)
            def _():
                copy.wait_send()
        for i in range(3):
            for j in range(3):
                there = (
                    (a >= fx) & (b >= fy) & (3 * (a - fx) + i < cx) & (3 * (b - fy) + j < cy)
                )

                @pl.when(there)
                def _():
                    for c in (1, 2, 0):
                        piece = fb.at[3 * i + j, c]
                        pltpu.make_async_remote_copy(
                            src_ref=piece, dst_ref=piece, send_sem=fb_send.at[c],
                            recv_sem=fb_recv.at[3 * i + j, c], device_id=(g, a, b),
                            device_id_type=MESH,
                        ).wait_recv()
                        at = (c, slice(XB + i * tx, XB + (i + 1) * tx),
                              slice(YB + j * ty, YB + (j + 1) * ty), slice(None))
                        now = S[at]
                        S[at] = now + FEEDBACK * (piece[...] - now)

    store = pltpu.make_async_copy(S.at[:, pl.ds(XB, nx), pl.ds(YB, ny), :], out.at[0], out_sem)
    store.start()
    for k in range(SUBS):
        for d in range(4):
            @pl.when(dirs[d][0])
            def _():
                halo_copy(k, d).wait_send()
    store.wait()


def per_device(
    state, courant, vert_inverse, interp_index, interp_weight, restrict_index, restrict_weight
):
    cx, cy = lax.axis_size("gx"), lax.axis_size("gy")
    _, _, nx, ny, lev = state.shape
    tx, ty = nx // 3, ny // 3
    vmem = lambda *shape: pltpu.VMEM(shape, F32)
    dma = pltpu.SemaphoreType.DMA
    anywhere = pl.BlockSpec(memory_space=pl.ANY)
    inside = pl.BlockSpec(memory_space=pltpu.VMEM)
    return pl.pallas_call(
        functools.partial(kernel, cx, cy),
        out_shape=jax.ShapeDtypeStruct(state.shape, F32),
        in_specs=[anywhere, anywhere] + [inside] * 5,
        out_specs=anywhere,
        scratch_shapes=[
            vmem(3, nx + 4, ny + 16, lev),
            vmem(nx + 2, ny + 16, lev),
            vmem(3, nx, ny, lev),
            vmem(2, 4, ny, lev),
            vmem(2, nx, 4, lev),
            vmem(2, 4, ny, lev),
            vmem(2, nx, 4, lev),
            vmem(SUBS - 1, 2, 2, ny, lev),
            vmem(SUBS - 1, 2, nx, 2, lev),
            vmem(SUBS - 1, 2, 2, ny, lev),
            vmem(SUBS - 1, 2, nx, 2, lev),
            vmem(3, tx, ty, lev),
            vmem(9, 3, tx, ty, lev),
            vmem(3, 3, ty + 16, lev),
            vmem(3, tx + 2, 8, lev),
            dma((2,)),
            dma((SUBS, 4)),
            dma((SUBS, 4)),
            dma((2, 2, 5)),
            dma((2, 3)),
            dma((3,)),
            dma((9, 3)),
            dma,
        ],
        compiler_params=pltpu.CompilerParams(has_side_effects=True),
        name="nest_step",
    )(state, courant, vert_inverse, interp_index, interp_weight, restrict_index, restrict_weight)


def solution(mesh):
    return jax.shard_map(
        per_device,
        mesh=mesh,
        in_specs=(
            P("grp", None, "gx", "gy", None),
            P("grp", "gx", "gy", None),
            P("grp", None, None),
            P("gx", "gy", None),
            P("gx", "gy", None),
            P("gx", "gy", None),
            P("gx", "gy", None),
        ),
        out_specs=P("grp", None, "gx", "gy", None),
        check_vma=False,
    )
```

profile of v0, /device:TPU:20, one launch (start us, length us, event | category | flops | bytes accessed | tf_op | source)
XLA Modules:
  0.0 72.8 jit_solution(14847001731660415755)
XLA Ops:
  0.0 1.4 %copy.8.inverse = f32[1,90,90]{2,1,0:T(8,128)} copy(f32[1,90,90]{2,0,1:T(1,128)} %param.9) | data formatting | bytes 64800 | tf_op args[2]
  1.4 1.7 %copy.11.ridx = s32[12,16,9]{2,1,0:T(8,128)} copy(s32[12,16,9]{1,0,2:T(8,128)} %param.12) | data formatting | bytes 13824 | tf_op args[5]
  3.1 1.7 %copy.12.rwgt = f32[12,16,9]{2,1,0:T(8,128)} copy(f32[12,16,9]{1,0,2:T(8,128)} %param.13) | data formatting | bytes 13824 | tf_op args[6]
  4.7 2.2 %copy.9.iidx = s32[36,48,4]{2,1,0:T(8,128)} copy(s32[36,48,4]{1,2,0:T(4,128)} %param.10) | data formatting | bytes 55296 | tf_op args[3]
  6.9 2.2 %copy.10.iwgt = f32[36,48,4]{2,1,0:T(8,128)} copy(f32[36,48,4]{1,2,0:T(4,128)} %param.11) | data formatting | bytes 55296 | tf_op args[4]
  9.1 60.3 %nest_step.1 = f32[1,3,36,48,90]{4,3,2,1,0:T(8,128)} custom-call(f32[1,3,36,48,90]{4,3,2,1,0:T(8,128)} %state.1, f32[1,36,48,90]{3,2,1,0:T(8,128)} %courant.1, f32[1,90,90]{2,1,0:T(8,128)} %copy.8.inverse, s32[36,48,4]{2,1,0:T(8,128)} %copy.9.iidx, f32[36,48,4]{2,1,0:T(8,128)} %copy.10.iwgt, s32[12,16,9]{2,1,0:T(8,128)} %copy.11.ridx, f32[12,16,9]{2,1,0:T(8,128)} %copy.12.rwgt), custom_call_target="tpu_custom_call" | custom-call | tf_op jit(solution)/shard_map/nest_step/pallas_call | solution.py:463
  69.4 3.4 %copy.14 = f32[1,3,36,48,90]{4,3,2,1,0:T(8,128)} copy(f32[1,3,36,48,90]{4,3,2,1,0:T(8,128)} %nest_step.1) | data formatting | bytes 3732480
where the time goes:
time: 73.2 us; the launch traced here: 72.8 us
  Pallas kernels  60.3 us (82%)
  local copies, waits for them, and re-layouts  12.5 us (17%)
    pallas_call x1, Pallas kernels, per_device(): pl.pallas_call(functools.partial(kernel, cx, cy), out_shape=jax.ShapeDtyp...  60.3 us
    unnamed x6, local copies, waits for them, and re-layouts  12.5 us

commit v1 on v0

--- a/solution.py
+++ b/solution.py
@@ -33,25 +33,60 @@
     return (t * 11) >> 5
 
 
-def dense(cell, share, depth):
-    lanes = lax.broadcasted_iota(jnp.int32, (cell.shape[0], depth), 1)
-    total = jnp.zeros(lanes.shape, F32)
-    for k in range(cell.shape[1]):
-        total = total + jnp.where(lanes == cell[:, k : k + 1], share[:, k : k + 1], 0.0)
-    return total
+def dense(cells, shares, depth):
+    places = lax.broadcasted_iota(jnp.int32, (depth, cells[0].shape[1]), 0)
+    total = jnp.zeros(places.shape, F32)
+    for cell, share in zip(cells, shares):
+        total = total + jnp.where(places == cell, share, 0.0)
+    return total.T
 
 
 def kernel(
     cx, cy,
     state, courant, inverse, iidx, iwgt, ridx, rwgt,
-    out,
-    S, C, mean, sx0, sy0, rx0, ry0, sx, sy, rx, ry, rst, fb, xstrip, ystrip,
-    load_sem, halo_send, halo_recv, strip_send, strip_recv, fb_send, fb_recv, out_sem,
+    S,
+    C, mean, wr, wx, wy, sx0, sy0, rx0, ry0, sx, sy, rx, ry, rst, fb, xstrip, ystrip,
+    load_sem, halo_send, halo_recv, strip_send, strip_recv, fb_send, fb_recv,
 ):
     g, a, b = lax.axis_index("grp"), lax.axis_index("gx"), lax.axis_index("gy")
     nx, ny, lev = state.shape[2], state.shape[3], state.shape[4]
     tx, ty = nx // 3, ny // 3
     fx, fy = cx // 2, cy // 2
+
+    barrier = pltpu.get_barrier_semaphore()
+    greeted = []
+
+    def greet(on, device):
+        greeted.append(on)
+
+        @pl.when(on)
+        def _():
+            pl.semaphore_signal(barrier, inc=1, device_id=device, device_id_type=MESH)
+
+    greet(a > 0, (g, a - 1, b))
+    greet(a < cx - 1, (g, a + 1, b))
+    greet(b > 0, (g, a, b - 1))
+    greet(b < cy - 1, (g, a, b + 1))
+    for i in range(-1, 4):
+        for j in range(-1, 4):
+            child_a, child_b = 3 * (a - fx) + i, 3 * (b - fy) + j
+            greet(
+                (g == 0) & (a >= fx) & (b >= fy) & (child_a >= 0) & (child_a < cx)
+                & (child_b >= 0) & (child_b < cy),
+                (1, child_a, child_b),
+            )
+
+    def parents(place, first, count):
+        own = first + place // 3
+        return (
+            (place >= 0, own),
+            ((place % 3 == 0) & (place > 0), own - 1),
+            ((place % 3 == 2) & (own + 1 < count), own + 1),
+        )
+
+    for on_a, parent_a in parents(a, fx, cx):
+        for on_b, parent_b in parents(b, fy, cy):
+            greet((g == 1) & on_a & on_b, (0, parent_a, parent_b))
 
     loads = [
         pltpu.make_async_copy(
@@ -76,9 +111,10 @@
         S[c, XB : XB + nx, YB + ny : YB + ny + 8, :] = zcol
     C[1 : 1 + nx, 0:YB, :] = zcol
     C[1 : 1 + nx, YB + ny : YB + ny + 8, :] = zcol
-    m_high, m_low = split(inverse[0])
+    m_high, m_low = split(inverse[:, 0, :])
     for copy in loads:
         copy.wait()
+    pl.semaphore_wait(barrier, sum(on.astype(jnp.int32) for on in greeted))
 
     dirs = (
         (a > 0, a < cx - 1, (g, a - 1, b)),
@@ -126,6 +162,10 @@
             @pl.when(dirs[d][0])
             def _():
                 halo_copy(k, d).start()
+        if k == 0:
+            @pl.when(g == 1)
+            def _():
+                weights()
         for d in range(4):
             @pl.when(dirs[d][1])
             def _():
@@ -172,7 +212,7 @@
         lax.fori_loop(0, nx, row, 0)
 
     def press(k):
-        group = 4
+        group = 12
 
         def rows(i, _):
             parts = []
@@ -204,12 +244,7 @@
 
     def restrict(comps):
         def row(u, _):
-            t = ridx[u]
-            w = rwgt[u]
-            share = w * (1.0 / SUBS) / jnp.sum(w, axis=-1, keepdims=True)
-            over = third(t)
-            cell = over * ny + (t - 3 * over) + 3 * lax.broadcasted_iota(jnp.int32, t.shape, 0)
-            w_high, w_low = split(dense(cell, share, 3 * ny))
+            w_high, w_low = split(wr[u])
             for c in comps:
                 block = mean[c, pl.ds(3 * u, 3)].reshape(3 * ny, lev)
                 b_high, b_low = split(block)
@@ -217,6 +252,78 @@
             return 0
 
         lax.fori_loop(0, tx, row, 0)
+
+    def row_sum(rows):
+        total = rows[0]
+        for row in rows[1:]:
+            total = total + row
+        return total
+
+    def weights():
+        x_low, x_high = a == 0, a == cx - 1
+        y_low, y_high = b == 0, b == cy - 1
+
+        def restrict_row(u, _):
+            terms = range(ridx.shape[0])
+            w = [rwgt[k, pl.ds(u, 1), :] for k in terms]
+            scale = (1.0 / SUBS) / row_sum(w)
+            over = [third(ridx[k, pl.ds(u, 1), :]) for k in terms]
+            v3 = 3 * lax.broadcasted_iota(jnp.int32, (1, ty), 1)
+            cells = [
+                over[k] * (ny - 3) + ridx[k, pl.ds(u, 1), :] + v3 for k in terms
+            ]
+            wr[u] = dense(cells, [part * scale for part in w], 3 * ny)
+            return 0
+
+        lax.fori_loop(0, tx, restrict_row, 0)
+
+        def boundary_row(x, cols, origin_x, origin_y, width, depth):
+            w = [iwgt[x, k : k + 1, cols] for k in range(4)]
+            scale = 1.0 / row_sum(w)
+            y = cols.start + lax.broadcasted_iota(jnp.int32, w[0].shape, 1)
+            y3 = (y * 171) >> 9
+            cells = []
+            for k in range(4):
+                t = iidx[x, k : k + 1, cols]
+                over = third(t)
+                source_x = jnp.clip(a * tx + x // 3 + over - 1, 0, cx * tx - 1) - origin_x
+                source_y = jnp.clip(b * ty + y3 + (t - 3 * over) - 1, 0, cy * ty - 1) - origin_y
+                cells.append(source_x * width + source_y)
+            return dense(cells, [part * scale for part in w], depth)
+
+        def y_weights(col, strip0):
+            def row(x, _):
+                wy[x] = boundary_row(
+                    x, slice(col, col + 8), a * tx + x // 3 - 1, b * ty + strip0, 8, 24
+                )
+                return 0
+
+            lax.fori_loop(0, nx, row, 0)
+
+        def x_weights(first, strip0):
+            def row(i, _):
+                wx[i] = boundary_row(
+                    first + i, slice(0, ny), a * tx + strip0, b * ty - 8, ty + 16, 3 * (ty + 16)
+                )
+                return 0
+
+            lax.fori_loop(0, BAND, row, 0)
+
+        @pl.when(y_low)
+        def _():
+            y_weights(0, 0)
+
+        @pl.when(y_high)
+        def _():
+            y_weights(ny - 8, ty - 8)
+
+        @pl.when(x_low)
+        def _():
+            x_weights(0, 0)
+
+        @pl.when(x_high)
+        def _():
+            x_weights(nx - BAND, tx - 3)
 
     for k in range(SUBS):
         exchange(k)
@@ -293,22 +400,11 @@
         ).astype(F32)
         return jnp.maximum(1.0 - depth / BAND, 0.0)
 
-    def shares_of(w):
-        return w / jnp.sum(w, axis=-1, keepdims=True)
-
-    def y_edge(col, strip0):
+    def y_edge(col):
         def row(u, _):
-            t = iidx[pl.ds(3 * u, 3), pl.ds(col, 8), :].reshape(24, 4)
-            share = shares_of(iwgt[pl.ds(3 * u, 3), pl.ds(col, 8), :].reshape(24, 4))
-            over = third(t)
-            n = lax.broadcasted_iota(jnp.int32, (24, 4), 0)
-            source_x = jnp.clip(a * tx + u + over - 1, 0, cx * tx - 1) - (a * tx + u - 1)
-            y = col + (n & 7)
-            y3 = (y * 171) >> 9
-            source_y = jnp.clip(b * ty + y3 + (t - 3 * over) - 1, 0, cy * ty - 1) - (b * ty + strip0)
-            w_high, w_low = split(dense(source_x * 8 + source_y, share, 24))
             n = lax.broadcasted_iota(jnp.int32, (24, lev), 0)
             relax = relax_at(3 * u + (n >> 3), col + (n & 7))
+            w_high, w_low = split(wy[pl.ds(3 * u, 3)].reshape(24, 24))
             for c in range(3):
                 s_high, s_low = split(ystrip[c, pl.ds(u, 3)].reshape(24, lev))
                 bound = dot(w_high, s_high) + (dot(w_low, s_high) + dot(w_high, s_low))
@@ -319,27 +415,18 @@
 
         lax.fori_loop(0, tx, row, 0)
 
-    def x_edge(first, strip0):
+    def x_edge(first):
         def row(i, _):
             x = first + i
-            t = iidx[x]
-            share = shares_of(iwgt[x])
-            over = third(t)
-            source_x = jnp.clip(a * tx + x // 3 + over - 1, 0, cx * tx - 1) - (a * tx + strip0)
-            y = lax.broadcasted_iota(jnp.int32, (ny, 4), 0)
-            y3 = (y * 171) >> 9
-            source_y = jnp.clip(b * ty + y3 + (t - 3 * over) - 1, 0, cy * ty - 1) - (b * ty - 8)
-            w_high, w_low = split(dense(source_x * (ty + 16) + source_y, share, 3 * (ty + 16)))
-            y = lax.broadcasted_iota(jnp.int32, (ny, lev), 0)
-            relax = relax_at(x, y)
+            w_high, w_low = split(wx[i])
+            relax = relax_at(x, lax.broadcasted_iota(jnp.int32, (ny, lev), 0))
             for c in range(3):
                 s_high, s_low = split(xstrip[c].reshape(3 * (ty + 16), lev))
                 bound = dot(w_high, s_high) + (dot(w_low, s_high) + dot(w_high, s_low))
-                now = keep[c, i]
+                now = mean[c, i]
                 S[c, XB + x, YB : YB + ny, :] = now + relax * (bound - now)
             return 0
 
-        keep = mean
         lax.fori_loop(0, BAND, row, 0)
 
     @pl.when(g == 1)
@@ -389,11 +476,11 @@
 
         @pl.when(y_low)
         def _():
-            y_edge(0, 0)
+            y_edge(0)
 
         @pl.when(y_high)
         def _():
-            y_edge(ny - 8, ty - 8)
+            y_edge(ny - 8)
 
         @pl.when(x_low | x_high)
         def _():
@@ -401,11 +488,11 @@
 
         @pl.when(x_low)
         def _():
-            x_edge(0, 0)
+            x_edge(0)
 
         @pl.when(x_high)
         def _():
-            x_edge(nx - BAND, tx - 3)
+            x_edge(nx - BAND)
 
         for c in range(3):
             fb_copy(c).wait_send()
@@ -440,14 +527,11 @@
                         now = S[at]
                         S[at] = now + FEEDBACK * (piece[...] - now)
 
-    store = pltpu.make_async_copy(S.at[:, pl.ds(XB, nx), pl.ds(YB, ny), :], out.at[0], out_sem)
-    store.start()
     for k in range(SUBS):
         for d in range(4):
             @pl.when(dirs[d][0])
             def _():
                 halo_copy(k, d).wait_send()
-    store.wait()
 
 
 def per_device(
@@ -458,17 +542,19 @@
     tx, ty = nx // 3, ny // 3
     vmem = lambda *shape: pltpu.VMEM(shape, F32)
     dma = pltpu.SemaphoreType.DMA
-    anywhere = pl.BlockSpec(memory_space=pl.ANY)
+    anywhere = pl.BlockSpec(memory_space=pltpu.HBM)
     inside = pl.BlockSpec(memory_space=pltpu.VMEM)
-    return pl.pallas_call(
+    padded = pl.pallas_call(
         functools.partial(kernel, cx, cy),
-        out_shape=jax.ShapeDtypeStruct(state.shape, F32),
+        out_shape=vmem(3, nx + 4, ny + 16, lev),
         in_specs=[anywhere, anywhere] + [inside] * 5,
-        out_specs=anywhere,
+        out_specs=inside,
         scratch_shapes=[
-            vmem(3, nx + 4, ny + 16, lev),
             vmem(nx + 2, ny + 16, lev),
             vmem(3, nx, ny, lev),
+            vmem(tx, ty, 3 * ny),
+            vmem(BAND, ny, 3 * (ty + 16)),
+            vmem(nx, 8, 24),
             vmem(2, 4, ny, lev),
             vmem(2, nx, 4, lev),
             vmem(2, 4, ny, lev),
@@ -488,11 +574,17 @@
             dma((2, 3)),
             dma((3,)),
             dma((9, 3)),
-            dma,
         ],
-        compiler_params=pltpu.CompilerParams(has_side_effects=True),
+        compiler_params=pltpu.CompilerParams(
+            has_side_effects=True, collective_id=0, vmem_limit_bytes=44 * 2**20
+        ),
         name="nest_step",
-    )(state, courant, vert_inverse, interp_index, interp_weight, restrict_index, restrict_weight)
+    )(
+        state, courant, vert_inverse.transpose(1, 0, 2),
+        interp_index.transpose(0, 2, 1), interp_weight.transpose(0, 2, 1),
+        restrict_index.transpose(2, 0, 1), restrict_weight.transpose(2, 0, 1),
+    )
+    return padded[None, :, XB : XB + nx, YB : YB + ny, :]
 
 
 def solution(mesh):

time: 73.2 us -> 62.5 us (0.85)
  Pallas kernels: 60.3 us -> 53.1 us
  local copies, waits for them, and re-layouts: 12.5 us -> 8.97 us
    pallas_call x1, Pallas kernels: 60.3 us -> 53.1 us  [per_device(): pl.pallas_call(functools.partial(kernel, cx, cy), out_shape=vmem(3, nx +...]
    unnamed x6 -> x14, local copies, waits for them, and re-layouts: 12.5 us -> 7.24 us
    broadcast_in_dim x0 -> x1, local copies, waits for them, and re-layouts: none -> 1.73 us  [per_device(): return padded[None, :, XB:XB + nx, YB:YB + ny, :]]
where the time goes in v1:
time: 62.5 us; the launch traced here: 62.1 us
  Pallas kernels  53.1 us (85%)
  local copies, waits for them, and re-layouts  8.97 us (14%)
    pallas_call x1, Pallas kernels, per_device(): pl.pallas_call(functools.partial(kernel, cx, cy), out_shape=vmem(3, nx +...  53.1 us
    unnamed x14, local copies, waits for them, and re-layouts  7.24 us
    broadcast_in_dim x1, local copies, waits for them, and re-layouts, per_device(): return padded[None, :, XB:XB + nx, YB:YB + ny, :]  1.73 us

profile of v1, /device:TPU:20, one launch (start us, length us, event | category | flops | bytes accessed | tf_op | source)
XLA Modules:
  0.0 62.1 jit_solution(13498542898770883783)
XLA Ops:
  0.0 0.0 copy-start
  0.0 1.7 %copy-done = f32[1,3,36,48,90]{4,3,2,1,0:T(8,128)S(1)} copy-done((f32[1,3,36,48,90]{4,3,2,1,0:T(8,128)S(1)}, f32[1,3,36,48,90]{4,3,2,1,0:T(8,128)}, u32[]{:S(2)}) %copy-start) | copy-done | bytes 1866264
  1.8 0.0 copy-start.1
  1.8 1.2 %copy-done.1 = f32[1,36,48,90]{3,2,1,0:T(8,128)S(1)} copy-done((f32[1,36,48,90]{3,2,1,0:T(8,128)S(1)}, f32[1,36,48,90]{3,2,1,0:T(8,128)}, u32[]{:S(2)}) %copy-start.1) | copy-done | bytes 622104
  2.9 0.0 copy-start.2
  2.9 0.9 %copy-done.2 = s32[36,48,4]{1,2,0:T(4,128)S(1)} copy-done((s32[36,48,4]{1,2,0:T(4,128)S(1)}, s32[36,48,4]{1,2,0:T(4,128)}, u32[]{:S(2)}) %copy-start.2) | copy-done | bytes 27672
  3.8 0.0 copy-start.3
  3.8 0.9 %copy-done.3 = f32[36,48,4]{1,2,0:T(4,128)S(1)} copy-done((f32[36,48,4]{1,2,0:T(4,128)S(1)}, f32[36,48,4]{1,2,0:T(4,128)}, u32[]{:S(2)}) %copy-start.3) | copy-done | bytes 27672
  4.7 0.0 copy-start.4
  4.7 0.9 %copy-done.4 = s32[12,16,9]{1,0,2:T(8,128)S(1)} copy-done((s32[12,16,9]{1,0,2:T(8,128)S(1)}, s32[12,16,9]{1,0,2:T(8,128)}, u32[]{:S(2)}) %copy-start.4) | copy-done | bytes 6936
  5.6 0.0 copy-start.5
  5.6 0.9 %copy-done.5 = f32[12,16,9]{1,0,2:T(8,128)S(1)} copy-done((f32[12,16,9]{1,0,2:T(8,128)S(1)}, f32[12,16,9]{1,0,2:T(8,128)}, u32[]{:S(2)}) %copy-start.5) | copy-done | bytes 6936
  6.5 0.0 copy-start.6
  6.5 0.8 %copy-done.6 = f32[1,90,90]{2,0,1:T(1,128)S(1)} copy-done((f32[1,90,90]{2,0,1:T(1,128)S(1)}, f32[1,90,90]{2,0,1:T(1,128)}, u32[]{:S(2)}) %copy-start.6) | copy-done | bytes 32424
  7.2 53.1 %nest_step.1 = f32[3,40,64,90]{3,2,1,0:T(8,128)S(1)} custom-call(f32[1,3,36,48,90]{4,3,2,1,0:T(8,128)S(1)} %copy-done, f32[1,36,48,90]{3,2,1,0:T(8,128)S(1)} %copy-done.1, f32[90,1,90]{2,1,0:T(1,128)S(1)} %bitcast.11, s32[36,4,48]{2,1,0:T(4,128)S(1)} %bitcast.7, f32[36,4,48]{2,1,0:T(4,128)S(1)} %bitcast.8, s32[9,12,16]{2,1,0:T(8,128)S(1)} %bitcast.9, ...), custom_call_target="tpu_custom_call" | custom-call | tf_op jit(solution)/shard_map/nest_step/pallas_call | solution.py:547
  60.4 1.7 %slice_bitcast_fusion = f32[1,3,36,48,90]{4,3,2,1,0:T(8,128)} fusion(f32[3,40,64,90]{3,2,1,0:T(8,128)S(1)} %nest_step.1), kind=kLoop, calls=%fused_computation | loop fusion | bytes 3732480 | tf_op jit(solution)/shard_map/broadcast_in_dim | solution.py:587
Async XLA Ops:
  0.0 1.7 %copy-start = (f32[1,3,36,48,90]{4,3,2,1,0:T(8,128)S(1)}, f32[1,3,36,48,90]{4,3,2,1,0:T(8,128)}, u32[]{:S(2)}) copy-start(f32[1,3,36,48,90]{4,3,2,1,0:T(8,128)} %state.1) | copy-start | bytes 5598724
  1.8 1.2 %copy-start.1 = (f32[1,36,48,90]{3,2,1,0:T(8,128)S(1)}, f32[1,36,48,90]{3,2,1,0:T(8,128)}, u32[]{:S(2)}) copy-start(f32[1,36,48,90]{3,2,1,0:T(8,128)} %courant.1) | copy-start | bytes 1866244
  2.9 0.9 %copy-start.2 = (s32[36,48,4]{1,2,0:T(4,128)S(1)}, s32[36,48,4]{1,2,0:T(4,128)}, u32[]{:S(2)}) copy-start(s32[36,48,4]{1,2,0:T(4,128)} %param.10) | copy-start | bytes 82948
  3.8 0.9 %copy-start.3 = (f32[36,48,4]{1,2,0:T(4,128)S(1)}, f32[36,48,4]{1,2,0:T(4,128)}, u32[]{:S(2)}) copy-start(f32[36,48,4]{1,2,0:T(4,128)} %param.11) | copy-start | bytes 82948
  4.7 0.9 %copy-start.4 = (s32[12,16,9]{1,0,2:T(8,128)S(1)}, s32[12,16,9]{1,0,2:T(8,128)}, u32[]{:S(2)}) copy-start(s32[12,16,9]{1,0,2:T(8,128)} %param.12) | copy-start | bytes 20740
  5.6 0.9 %copy-start.5 = (f32[12,16,9]{1,0,2:T(8,128)S(1)}, f32[12,16,9]{1,0,2:T(8,128)}, u32[]{:S(2)}) copy-start(f32[12,16,9]{1,0,2:T(8,128)} %param.13) | copy-start | bytes 20740
  6.5 0.8 %copy-start.6 = (f32[1,90,90]{2,0,1:T(1,128)S(1)}, f32[1,90,90]{2,0,1:T(1,128)}, u32[]{:S(2)}) copy-start(f32[1,90,90]{2,0,1:T(1,128)} %param.9) | copy-start | bytes 97204

commit v2 on v1

--- a/solution.py
+++ b/solution.py
@@ -43,11 +43,14 @@
 
 def kernel(
     cx, cy,
-    state, courant, inverse, iidx, iwgt, ridx, rwgt,
+    state, courant, *rest,
+):
+    small, (
     S,
-    C, mean, wr, wx, wy, sx0, sy0, rx0, ry0, sx, sy, rx, ry, rst, fb, xstrip, ystrip,
+    C, inverse, iidx, iwgt, ridx, rwgt, mean, wr, wx, wy, sx0, sy0, rx0, ry0, sx, sy, rx, ry, rst, fb, xstrip, ystrip,
     load_sem, halo_send, halo_recv, strip_send, strip_recv, fb_send, fb_recv,
-):
+    q0, q1, q2, q3, q_send, q_recv,
+    ) = rest[:5], rest[5:]
     g, a, b = lax.axis_index("grp"), lax.axis_index("gx"), lax.axis_index("gy")
     nx, ny, lev = state.shape[2], state.shape[3], state.shape[4]
     tx, ty = nx // 3, ny // 3
@@ -88,6 +91,52 @@
         for on_b, parent_b in parents(b, fy, cy):
             greet((g == 1) & on_a & on_b, (0, parent_a, parent_b))
 
+    def route(at_a, at_b):
+        to_a, to_b = fx + at_a // 3, fy + at_b // 3
+        far = (at_a != to_a) & (at_b != to_b)
+        direct = (at_a == to_a) & (at_b == to_b)
+        by_nest = (at_a % 3 == 1) & (at_b == to_b) & (at_a != to_a)
+        over = jnp.logical_not(direct | by_nest)
+        along_a = over & (at_a % 3 == 1) & far
+        along_b = over & (at_a % 3 == 0) & far
+        last = over & jnp.logical_not(along_a | along_b)
+        return to_a, to_b, direct, by_nest, over, along_a, along_b, last
+
+    to_a, to_b, direct, by_nest, over, along_a, along_b, last = route(a, b)
+    parent, nest = g == 0, g == 1
+    mid_a = 3 * (a - fx) + 1
+    comes = (a >= fx) & (mid_a < cx)
+    middle = route(mid_a, b)
+    relay1, relay3 = parent & comes & middle[5], nest & comes & middle[3]
+    relay2 = []
+    for j in range(3):
+        side_b = 3 * (b - fy) + j
+        relay2.append((parent & (b >= fy) & (side_b < cy) & route(a, side_b)[6], side_b))
+    greet(nest & over, (0, a, b))
+    greet(parent & over, (1, a, b))
+    greet(parent & along_a, (0, to_a, b))
+    greet(relay1, (0, mid_a, b))
+    greet(parent & along_b, (0, a, to_b))
+    for on, side_b in relay2:
+        greet(on, (0, a, side_b))
+        greet(on, (0, to_a, b))
+    greet(nest & by_nest, (1, to_a, b))
+    greet(relay3, (1, mid_a, b))
+    greet(parent & last, (0, to_a, to_b))
+    greet(relay1, (0, a, to_b))
+    greet(relay3, (0, a, b))
+    greet(nest & direct, (0, a, b))
+    for i in range(3):
+        for j in range(3):
+            from_a, from_b = 3 * (a - fx) + i, 3 * (b - fy) + j
+            on = parent & (a >= fx) & (b >= fy) & (from_a < cx) & (from_b < cy)
+            _, _, f_direct, f_nest, _, f_a, f_b, f_last = route(from_a, from_b)
+            greet(on & f_direct, (1, a, b))
+            greet(on & f_nest, (1, a, from_b))
+            greet(on & f_a, (0, a, from_b))
+            greet(on & f_b, (0, from_a, b))
+            greet(on & f_last, (0, from_a, from_b))
+
     loads = [
         pltpu.make_async_copy(
             state.at[0], S.at[:, pl.ds(XB, nx), pl.ds(YB, ny), :], load_sem.at[0]
@@ -96,6 +145,8 @@
             courant.at[0], C.at[pl.ds(1, nx), pl.ds(YB, ny), :], load_sem.at[1]
         ),
     ]
+    for n, (src, dst) in enumerate(zip(small, (inverse, iidx, iwgt, ridx, rwgt))):
+        loads.append(pltpu.make_async_copy(src, dst, load_sem.at[2 + n]))
     for copy in loads:
         copy.start()
     zrow = jnp.zeros((2, ny, lev), F32)
@@ -111,9 +162,9 @@
         S[c, XB : XB + nx, YB + ny : YB + ny + 8, :] = zcol
     C[1 : 1 + nx, 0:YB, :] = zcol
     C[1 : 1 + nx, YB + ny : YB + ny + 8, :] = zcol
-    m_high, m_low = split(inverse[:, 0, :])
     for copy in loads:
         copy.wait()
+    m_high, m_low = split(inverse[:, 0, :])
     pl.semaphore_wait(barrier, sum(on.astype(jnp.int32) for on in greeted))
 
     dirs = (
@@ -233,14 +284,66 @@
 
         lax.fori_loop(0, nx // group, rows, 0)
 
-    slot = (a % 3) * 3 + b % 3
-
-    def fb_copy(c):
+    def hop(src, dst, device, send, recv):
         return pltpu.make_async_remote_copy(
-            src_ref=rst.at[c], dst_ref=fb.at[slot, c],
-            send_sem=fb_send.at[c], recv_sem=fb_recv.at[slot, c],
-            device_id=(0, fx + a // 3, fy + b // 3), device_id_type=MESH,
+            src_ref=src, dst_ref=dst, send_sem=send, recv_sem=recv,
+            device_id=device, device_id_type=MESH,
         )
+
+    def home(src, c, i, j, device, send):
+        n = 3 * i + j
+        return hop(src, fb.at[n, c], device, send, fb_recv.at[n, c])
+
+    def fb_copies(c):
+        mine, sem = rst.at[c], fb_send.at[c]
+        return (
+            (direct, home(mine, c, a % 3, b % 3, (0, a, b), sem)),
+            (by_nest, hop(mine, q3.at[c], (1, to_a, b), sem, q_recv.at[5, c])),
+            (over, hop(mine, q0.at[c], (0, a, b), sem, q_recv.at[0, c])),
+        )
+
+    def fb_start(c):
+        for on, copy in fb_copies(c):
+            @pl.when(on)
+            def _():
+                copy.start()
+
+    def relays(c):
+        sem0 = q_send.at[0, c]
+        yield parent & over, q0.at[c], 0, (
+            (along_a, hop(q0.at[c], q1.at[c], (0, to_a, b), sem0, q_recv.at[1, c])),
+            (along_b, hop(q0.at[c], q2.at[b % 3, c], (0, a, to_b), sem0,
+                          q_recv.at[2 + b % 3, c])),
+            (last, home(q0.at[c], c, a % 3, b % 3, (0, to_a, to_b), sem0)),
+        )
+        yield relay1, q1.at[c], 1, (
+            (relay1, home(q1.at[c], c, 1, b % 3, (0, a, to_b), q_send.at[1, c])),
+        )
+        for j, (on, side_b) in enumerate(relay2):
+            yield on, q2.at[j, c], 2 + j, (
+                (on, home(q2.at[j, c], c, 0, j, (0, to_a, b), q_send.at[2 + j, c])),
+            )
+        yield relay3, q3.at[c], 5, (
+            (relay3, home(q3.at[c], c, 1, b % 3, (0, a, b), q_send.at[5, c])),
+        )
+
+    def pass_on():
+        for c in (1, 2, 0):
+            for here, buffer, n, onward in relays(c):
+                @pl.when(here)
+                def _():
+                    hop(buffer, buffer, (g, a, b), q_send.at[n, c], q_recv.at[n, c]).wait_recv()
+                    for on, copy in onward:
+                        @pl.when(on)
+                        def _():
+                            copy.start()
+
+    def passed_on():
+        for c in (1, 2, 0):
+            for here, buffer, n, onward in relays(c):
+                @pl.when(here)
+                def _():
+                    hop(buffer, buffer, (g, a, b), q_send.at[n, c], q_recv.at[n, c]).wait_send()
 
     def restrict(comps):
         def row(u, _):
@@ -332,8 +435,8 @@
             @pl.when(g == 1)
             def _():
                 restrict((1, 2))
-                fb_copy(1).start()
-                fb_copy(2).start()
+                fb_start(1)
+                fb_start(2)
         press(k)
 
     x_windows = {-1: (0, 8, 24), 0: (0, ty + 8, 8), 1: (ty - 8, 2 * ty + 8, 0),
@@ -432,7 +535,8 @@
     @pl.when(g == 1)
     def _():
         restrict((0,))
-        fb_copy(0).start()
+        fb_start(0)
+        pass_on()
         x_low, x_high = a == 0, a == cx - 1
         y_low, y_high = b == 0, b == cy - 1
 
@@ -495,7 +599,7 @@
             x_edge(nx - BAND)
 
         for c in range(3):
-            fb_copy(c).wait_send()
+            hop(rst.at[c], rst.at[c], (g, a, b), fb_send.at[c], q_recv.at[0, c]).wait_send()
 
     @pl.when(g == 0)
     def _():
@@ -503,6 +607,7 @@
             @pl.when(on)
             def _():
                 copy.start()
+        pass_on()
         for on, copy in strip_copies():
             @pl.when(on)
             def _():
@@ -532,6 +637,7 @@
             @pl.when(dirs[d][0])
             def _():
                 halo_copy(k, d).wait_send()
+    passed_on()
 
 
 def per_device(
@@ -547,10 +653,15 @@
     padded = pl.pallas_call(
         functools.partial(kernel, cx, cy),
         out_shape=vmem(3, nx + 4, ny + 16, lev),
-        in_specs=[anywhere, anywhere] + [inside] * 5,
+        in_specs=[anywhere] * 7,
         out_specs=inside,
         scratch_shapes=[
             vmem(nx + 2, ny + 16, lev),
+            vmem(lev, 1, lev),
+            pltpu.VMEM((nx, 4, ny), jnp.int32),
+            vmem(nx, 4, ny),
+            pltpu.VMEM((9, tx, ty), jnp.int32),
+            vmem(9, tx, ty),
             vmem(3, nx, ny, lev),
             vmem(tx, ty, 3 * ny),
             vmem(BAND, ny, 3 * (ty + 16)),
@@ -567,16 +678,22 @@
             vmem(9, 3, tx, ty, lev),
             vmem(3, 3, ty + 16, lev),
             vmem(3, tx + 2, 8, lev),
-            dma((2,)),
+            dma((7,)),
             dma((SUBS, 4)),
             dma((SUBS, 4)),
             dma((2, 2, 5)),
             dma((2, 3)),
             dma((3,)),
             dma((9, 3)),
+            vmem(3, tx, ty, lev),
+            vmem(3, tx, ty, lev),
+            vmem(3, 3, tx, ty, lev),
+            vmem(3, tx, ty, lev),
+            dma((6, 3)),
+            dma((6, 3)),
         ],
         compiler_params=pltpu.CompilerParams(
-            has_side_effects=True, collective_id=0, vmem_limit_bytes=44 * 2**20
+            has_side_effects=True, collective_id=0, vmem_limit_bytes=67043328 - 4 * (3 * (nx + 4) * (ny + 16) * 128) - 2**14
         ),
         name="nest_step",
     )(

time: 62.5 us -> 55.1 us (0.88)
  local copies, waits for them, and re-layouts: 8.97 us -> 1.73 us
    unnamed x14 -> x0, local copies, waits for them, and re-layouts: 7.24 us -> none
where the time goes in v2:
time: 55.1 us; the launch traced here: 55 us
  Pallas kernels  53.2 us (97%)
  local copies, waits for them, and re-layouts  1.73 us (3%)
    pallas_call x1, Pallas kernels, per_device(): pl.pallas_call(functools.partial(kernel, cx, cy), out_shape=vmem(3, nx +...  53.2 us
    broadcast_in_dim x1, local copies, waits for them, and re-layouts, per_device(): return padded[None, :, XB:XB + nx, YB:YB + ny, :]  1.73 us

profile of v2, /device:TPU:20, one launch (start us, length us, event | category | flops | bytes accessed | tf_op | source)
XLA Modules:
  0.0 55.0 jit_solution(12278715395797359908)
XLA Ops:
  0.0 53.2 %nest_step.1 = f32[3,40,64,90]{3,2,1,0:T(8,128)S(1)} custom-call(f32[1,3,36,48,90]{4,3,2,1,0:T(8,128)} %state.1, f32[1,36,48,90]{3,2,1,0:T(8,128)} %courant.1, f32[90,1,90]{2,1,0:T(1,128)} %bitcast.11, s32[36,4,48]{2,1,0:T(4,128)} %bitcast.7, f32[36,4,48]{2,1,0:T(4,128)} %bitcast.8, s32[9,12,16]{2,1,0:T(8,128)} %bitcast.9, f32[9,12,16]{2,1,0:T(8,128)} %bitcast.10), custom_call_target="tpu_custom_call" | custom-call | tf_op jit(solution)/shard_map/nest_step/pallas_call | solution.py:653
  53.2 1.7 %slice_bitcast_fusion = f32[1,3,36,48,90]{4,3,2,1,0:T(8,128)} fusion(f32[3,40,64,90]{3,2,1,0:T(8,128)S(1)} %nest_step.1), kind=kLoop, calls=%fused_computation | loop fusion | bytes 3732480 | tf_op jit(solution)/shard_map/broadcast_in_dim | solution.py:704

commit v3 on v2

--- a/solution.py
+++ b/solution.py
@@ -250,17 +250,27 @@
         u_row(XB - 1, 0)
         u_row(XB + nx, 0)
 
-        def row(x, _):
-            r = x + XB
-            u_row(r, 0)
-            add_mean(k, 1, x, S[1, r, YB : YB + ny, :])
-            wide = slice(YB - 1, YB + ny + 1)
-            slope = 0.5 * (S[0, r, YB : YB + ny + 2, :] - S[0, r, YB - 2 : YB + ny, :])
-            S[2, r, wide, :] = S[2, r, wide, :] - C[x + 1, wide, :] * slope
-            add_mean(k, 2, x, S[2, r, YB : YB + ny, :])
+        cols, wide = slice(YB, YB + ny), slice(YB - 1, YB + ny + 1)
+        group = 4
+
+        def rows(i, _):
+            new = []
+            for j in range(group):
+                x = i * group + j
+                r = x + XB
+                slope = 0.5 * (S[0, r + 1, cols, :] - S[0, r - 1, cols, :])
+                u = S[1, r, cols, :] - C[x + 1, cols, :] * slope
+                slope = 0.5 * (S[0, r, YB : YB + ny + 2, :] - S[0, r, YB - 2 : YB + ny, :])
+                v = S[2, r, wide, :] - C[x + 1, wide, :] * slope
+                new.append((x, u, v))
+            for x, u, v in new:
+                S[1, x + XB, cols, :] = u
+                S[2, x + XB, wide, :] = v
+                add_mean(k, 1, x, u)
+                add_mean(k, 2, x, v[1 : ny + 1])
             return 0
 
-        lax.fori_loop(0, nx, row, 0)
+        lax.fori_loop(0, nx // group, rows, 0)
 
     def press(k):
         group = 12
@@ -346,15 +356,23 @@
                     hop(buffer, buffer, (g, a, b), q_send.at[n, c], q_recv.at[n, c]).wait_send()
 
     def restrict(comps):
-        def row(u, _):
-            w_high, w_low = split(wr[u])
-            for c in comps:
-                block = mean[c, pl.ds(3 * u, 3)].reshape(3 * ny, lev)
-                b_high, b_low = split(block)
-                rst[c, u] = dot(w_high, b_high) + (dot(w_low, b_high) + dot(w_high, b_low))
+        group = 4
+
+        def rows(i, _):
+            new = []
+            for j in range(group):
+                u = i * group + j
+                w_high, w_low = split(wr[u])
+                for c in comps:
+                    block = mean[c, pl.ds(3 * u, 3)].reshape(3 * ny, lev)
+                    b_high, b_low = split(block)
+                    both = dot(w_high, b_high) + (dot(w_low, b_high) + dot(w_high, b_low))
+                    new.append((c, u, both))
+            for c, u, both in new:
+                rst[c, u] = both
             return 0
 
-        lax.fori_loop(0, tx, row, 0)
+        lax.fori_loop(0, tx // group, rows, 0)
 
     def row_sum(rows):
         total = rows[0]

time: 55.1 us -> 51.8 us (0.940)
  Pallas kernels: 53.2 us -> 49.9 us
    pallas_call x1, Pallas kernels: 53.2 us -> 49.9 us  [per_device(): pl.pallas_call(functools.partial(kernel, cx, cy), out_shape=vmem(3, nx +...]
where the time goes in v3:
time: 51.8 us; the launch traced here: 51.7 us
  Pallas kernels  49.9 us (96%)
  local copies, waits for them, and re-layouts  1.73 us (3%)
    pallas_call x1, Pallas kernels, per_device(): pl.pallas_call(functools.partial(kernel, cx, cy), out_shape=vmem(3, nx +...  49.9 us
    broadcast_in_dim x1, local copies, waits for them, and re-layouts, per_device(): return padded[None, :, XB:XB + nx, YB:YB + ny, :]  1.73 us

profile of v3, /device:TPU:20, one launch (start us, length us, event | category | flops | bytes accessed | tf_op | source)
XLA Modules:
  0.0 51.7 jit_solution(9315877748816676614)
XLA Ops:
  0.0 49.9 %nest_step.1 = f32[3,40,64,90]{3,2,1,0:T(8,128)S(1)} custom-call(f32[1,3,36,48,90]{4,3,2,1,0:T(8,128)} %state.1, f32[1,36,48,90]{3,2,1,0:T(8,128)} %courant.1, f32[90,1,90]{2,1,0:T(1,128)} %bitcast.11, s32[36,4,48]{2,1,0:T(4,128)} %bitcast.7, f32[36,4,48]{2,1,0:T(4,128)} %bitcast.8, s32[9,12,16]{2,1,0:T(8,128)} %bitcast.9, f32[9,12,16]{2,1,0:T(8,128)} %bitcast.10), custom_call_target="tpu_custom_call" | custom-call | tf_op jit(solution)/shard_map/nest_step/pallas_call | solution.py:671
  49.9 1.7 %slice_bitcast_fusion = f32[1,3,36,48,90]{4,3,2,1,0:T(8,128)} fusion(f32[3,40,64,90]{3,2,1,0:T(8,128)S(1)} %nest_step.1), kind=kLoop, calls=%fused_computation | loop fusion | bytes 3732480 | tf_op jit(solution)/shard_map/broadcast_in_dim | solution.py:722
